TPU v7x, 32 devices: a whole 2x2x4 slice. The times are simulated.
32 devices in a mesh: sys: 2 (over x), col: 4 (over z), seg: 4 (over y, core).
Axes of the slice: x: 2, y: 2, z: 4, core: 2. Of those that a mesh axis runs over, the one named last changes fastest.
Arguments:
- positions: bfloat16 [32768, 256], P(('sys', 'seg', 'col')), parts along dimension 0
- charges: float32 [32768], P(('sys', 'seg', 'col')), parts along dimension 0
Outputs:
- output 1: float32 [32768, 256], P(('sys', 'seg', 'col')), parts along dimension 0
- output 2: float32 [2], P('sys'), parts along dimension 0
There are 2 independent parts. A program takes and returns all parts, laid end to end along the dimension named above; each array names one.
All inputs are finite; a program needn't handle non-finite values.
Results may differ from a plain program's by a relative error of at most 0.001.
Values are sent between devices in bfloat16 or wider.
A program may use at most 1 GiB of HBM per device.

v0:
```python
import jax
import jax.numpy as jnp
from jax import lax
from jax.sharding import PartitionSpec as P

ROW_AXES = ('sys', 'seg', 'col')


def pair_weights(x_host, q_host, sq_host, x_vis, q_vis, inv_len2):
    sq_vis = jnp.sum(jnp.square(x_vis.astype(jnp.float32)), axis=1)
    dot_prod = lax.dot_general(x_host, x_vis, (((1,), (1,)), ((), ())), preferred_element_type=jnp.float32)
    sq_dist = jnp.maximum(sq_host[:, None] + sq_vis[None, :] - 2.0 * dot_prod, 0.0)
    return q_host[:, None] * q_vis[None, :] * jnp.exp(-0.5 * inv_len2 * sq_dist)


def host_terms(weights, w_low, x_host, x_vis):
    pulled = jnp.dot(w_low, x_vis, preferred_element_type=jnp.float32)
    return jnp.sum(weights, axis=1)[:, None] * x_host.astype(jnp.float32) - pulled


def visitor_terms(weights, w_low, x_host, x_vis):
    pushed = lax.dot_general(w_low, x_host, (((0,), (0,)), ((), ())), preferred_element_type=jnp.float32)
    return jnp.sum(weights, axis=0)[:, None] * x_vis.astype(jnp.float32) - pushed


def solution(mesh):
    seg_size = mesh.shape['seg']
    col_size = mesh.shape['col']
    far_step = seg_size // 2
    full_steps = (seg_size - 1) // 2
    forward = [(source, (source + 1) % seg_size) for source in range(seg_size)]
    back_home = [(source, (source - far_step) % seg_size) for source in range(seg_size)]

    def per_device(x_own, q_own):
        own_rows, feat_dim = x_own.shape
        inv_len2 = 1.0 / feat_dim
        team_rows = own_rows * col_size
        own_pos = lax.axis_index('col') * own_rows + jnp.arange(own_rows)
        team_pos = jnp.arange(team_rows)
        sq_own = jnp.sum(jnp.square(x_own.astype(jnp.float32)), axis=1)
        x_team = lax.all_gather(x_own, 'col', axis=0, tiled=True)
        q_team = lax.all_gather(q_own, 'col', axis=0, tiled=True)

        weights = pair_weights(x_own, q_own, sq_own, x_team, q_team, inv_len2)
        weights = jnp.where(own_pos[:, None] == team_pos[None, :], 0.0, weights)
        own_force = host_terms(weights, weights.astype(jnp.bfloat16), x_own, x_team)
        energy = 0.5 * jnp.sum(weights)

        def visit(x_vis, q_vis, reaction, own_force, energy, masked):
            weights = pair_weights(x_own, q_own, sq_own, x_vis, q_vis, inv_len2)
            if masked:
                low_half = lax.axis_index('seg') < far_step
                host_keep = jnp.where(low_half | (own_pos >= team_rows // 2), 1.0, 0.0)
                vis_keep = jnp.where(low_half & (team_pos >= team_rows // 2), 0.0, 1.0)
                weights = weights * host_keep[:, None] * vis_keep[None, :]
            w_low = weights.astype(jnp.bfloat16)
            own_force = own_force + host_terms(weights, w_low, x_own, x_vis)
            reaction = reaction + visitor_terms(weights, w_low, x_own, x_vis)
            return reaction, own_force, energy + jnp.sum(weights)

        x_vis = lax.ppermute(x_team, 'seg', forward)
        q_vis = lax.ppermute(q_team, 'seg', forward)
        reaction = jnp.zeros((team_rows, feat_dim), jnp.float32)
        reaction, own_force, energy = visit(x_vis, q_vis, reaction, own_force, energy, full_steps == 0)

        def step_body(step_idx, loop_state):
            x_vis, q_vis, reaction, own_force, energy = loop_state
            x_vis = lax.ppermute(x_vis, 'seg', forward)
            q_vis = lax.ppermute(q_vis, 'seg', forward)
            reaction = lax.ppermute(reaction, 'seg', forward)
            reaction, own_force, energy = visit(x_vis, q_vis, reaction, own_force, energy, False)
            return x_vis, q_vis, reaction, own_force, energy

        loop_state = lax.fori_loop(1, full_steps, step_body, (x_vis, q_vis, reaction, own_force, energy))
        x_vis, q_vis, reaction, own_force, energy = loop_state
        if 0 < full_steps < far_step:
            x_vis = lax.ppermute(x_vis, 'seg', forward)
            q_vis = lax.ppermute(q_vis, 'seg', forward)
            reaction = lax.ppermute(reaction, 'seg', forward)
            reaction, own_force, energy = visit(x_vis, q_vis, reaction, own_force, energy, True)

        reaction = lax.psum_scatter(reaction, 'col', scatter_dimension=0, tiled=True)
        reaction = lax.ppermute(reaction, 'seg', back_home)
        energy = lax.psum(energy, ('seg', 'col'))
        return (own_force + reaction) * inv_len2, energy.reshape(1)

    row_spec = P(ROW_AXES, None)
    return jax.shard_map(per_device, mesh=mesh, in_specs=(row_spec, P(ROW_AXES)), out_specs=(row_spec, P('sys')), check_vma=False)
```

profile of v0, /device:TPU:0, one launch (start us, length us, event | category | flops | bytes accessed | tf_op | source)
XLA Modules:
  0.0 307.0 jit_solution(203004505435363538)
XLA Ops:
  7.2 0.0 all-gather.2.cloned.1.call-start
  7.2 0.7 all-gather.2.cloned.1.call-update
  7.9 0.0 reduce-scatter.2.cloned.1.call-start
  7.9 49.7 %all-gather.2.cloned.1.call-done = bf16[4096,256]{1,0:T(8,128)(2,1)} async-done(((bf16[1024,256]{1,0:T(8,128)(2,1)}), bf16[4096,256]{1,0:T(8,128)(2,1)}) %all-gather.2.cloned.1.call-update) | async-done | bytes 2097168 | tf_op jit(solution)/shard_map/all_gather | solution.py:41
  57.6 0.0 collective-permute-start.1
  57.6 13.0 %all_gather.6 = f32[4096]{0:T(1024)S(1)} all-gather(f32[1024]{0:T(1024)} %param.3), channel_id=1, replica_groups=mesh['sys'=2,'col'=4,'seg'=4] {'col'}, dimensions={0}, use_global_device_ids=true | all-gather | bytes 20480 | tf_op jit(solution)/shard_map/all_gather | solution.py:42
  70.6 0.0 collective-permute-start
  70.6 1.3 fusion.18
  71.9 11.2 %collective-permute-done.1 = bf16[4096,256]{1,0:T(8,128)(2,1)} collective-permute-done((bf16[4096,256]{1,0:T(8,128)(2,1)}, bf16[4096,256]{1,0:T(8,128)(2,1)}, u32[]{:S(2)}, u32[]{:S(2)}) %collective-permute-start.1) | collective-permute-done | bytes 2097184 | tf_op jit(solution)/shard_map/ppermute | solution.py:61
  83.1 2.2 fusion.2
  85.3 0.0 copy-start
  85.3 0.1 collective-permute-start.3
  85.3 0.0 collective-permute-done
  85.4 11.1 %fusion.28 = (f32[]{:T(128)}, f32[4096]{0:T(1024)S(1)}, f32[1024]{0:T(1024)S(1)}, bf16[1024,4096]{1,0:T(8,128)(2,1)S(1)}) fusion(bf16[1024,256]{1,0:T(8,128)(2,1)} %param.2, bf16[4096,256]{1,0:T(8,128)(2,1)} %collective-permute-done.1, f32[4096]{0:T(1024)S(1)} %fusion.2, f32[1024]{0:T(1024)S(1)} %fusion.18, f32[4096]{0:T(1024)S(1)} %collective-permute-done, ...), kind=kOutput, calls=%fused_computation.42 | convolution fusion | flops 2193615872 | bytes 11071492 | tf_op jit(solution)/shard_map/dot_general | solution.py:11
  96.4 0.0 copy-start.4
  96.4 0.0 copy-done
  96.4 0.0 copy-start.3
  96.4 8.3 %fusion.3 = f32[4096,256]{1,0:T(8,128)} fusion(bf16[4096,256]{1,0:T(8,128)(2,1)} %collective-permute-done.1, f32[4096]{0:T(1024)S(1)} %get-tuple-element.6, bf16[1024,256]{1,0:T(8,128)(2,1)S(1)} %copy-done, bf16[1024,4096]{1,0:T(8,128)(2,1)S(1)} %get-tuple-element.10), kind=kOutput, calls=%fused_computation.11 | convolution fusion | flops 2150629376 | bytes 15220736 | tf_op jit(solution)/shard_map/dot_general | solution.py:22
  104.7 0.0 copy-done.4
  104.7 1.5 collective-permute-start.4
  106.2 0.3 collective-permute-start.2
  106.5 4.3 %collective-permute-done.3 = bf16[4096,256]{1,0:T(8,128)(2,1)S(1)} collective-permute-done((bf16[4096,256]{1,0:T(8,128)(2,1)}, bf16[4096,256]{1,0:T(8,128)(2,1)S(1)}, u32[]{:S(2)}, u32[]{:S(2)}) %collective-permute-start.3) | collective-permute-done | bytes 2097184 | tf_op jit(solution)/shard_map/ppermute | solution.py:77
  110.8 0.6 fusion.4
  111.4 44.5 %collective-permute-done.2 = f32[4096]{0:T(1024)S(1)} collective-permute-done((f32[4096]{0:T(1024)S(1)}, f32[4096]{0:T(1024)S(1)}, u32[]{:S(2)}, u32[]{:S(2)}) %collective-permute-start.2) | collective-permute-done | bytes 16416 | tf_op jit(solution)/shard_map/ppermute | solution.py:78
  155.9 0.0 copy-done.3
  155.9 10.4 %fusion.27 = (f32[]{:T(128)}, f32[4096]{0:T(1024)S(1)}, f32[1024]{0:T(1024)S(1)}, bf16[1024,4096]{1,0:T(8,128)(2,1)S(1)}) fusion(f32[4096]{0:T(1024)S(1)} %fusion.26, f32[1024]{0:T(1024)S(1)} %or_select_fusion, bf16[1024,256]{1,0:T(8,128)(2,1)S(1)} %copy-done, bf16[4096,256]{1,0:T(8,128)(2,1)S(1)} %collective-permute-done.3, f32[4096]{0:T(1024)S(1)} %fusion.4, ...), kind=kOutput, calls=%fused_computation.41 | convolution fusion | flops 2202004480 | bytes 11091972 | tf_op jit(solution)/shard_map/dot_general | solution.py:11
  166.3 0.0 copy-start.5
  166.3 2.7 fusion.7
  169.0 0.5 copy-done.5
  169.5 0.0 collective-permute-done.4
  169.5 4.0 %fusion.6 = f32[4096,256]{1,0:T(8,128)} fusion(f32[4096,256]{1,0:T(8,128)} %collective-permute-done.4, f32[4096,256]{1,0:T(8,128)S(1)} %fusion.7, bf16[4096,256]{1,0:T(8,128)(2,1)S(1)} %collective-permute-done.3, f32[4096]{0:T(1024)S(1)} %get-tuple-element.3), kind=kLoop, calls=%fused_computation.14 | loop fusion | flops 4194304 | bytes 14696448 | tf_op jit(solution)/shard_map/add | solution.py:58
  173.5 0.0 reduce-scatter.2.cloned.1.call-update
  173.5 2.2 multiply_reduce_fusion
  175.8 13.1 %fusion.29 = (f32[]{:T(128)}, f32[1024]{0:T(1024)S(1)}, bf16[1024,4096]{1,0:T(8,128)(2,1)}) fusion(bf16[1024,256]{1,0:T(8,128)(2,1)S(1)} %copy-done, bf16[4096,256]{1,0:T(8,128)(2,1)} %all-gather.2.cloned.1.call-done, f32[4096]{0:T(1024)S(1)} %multiply_reduce_fusion, f32[1024]{0:T(1024)S(1)} %fusion.18, f32[4096]{0:T(1024)S(1)} %all_gather.6, ...), kind=kOutput, calls=%fused_computation.43 | convolution fusion | flops 2197814272 | bytes 11059204 | tf_op jit(solution)/shard_map/dot_general | solution.py:11
  189.5 7.3 %fusion.15 = f32[1024,256]{1,0:T(8,128)} fusion(bf16[4096,256]{1,0:T(8,128)(2,1)} %all-gather.2.cloned.1.call-done, bf16[1024,4096]{1,0:T(8,128)(2,1)} %get-tuple-element.12, bf16[1024,256]{1,0:T(8,128)(2,1)S(1)} %copy-done, f32[1024]{0:T(1024)S(1)} %get-tuple-element.9), kind=kOutput, calls=%fused_computation.28 | convolution fusion | flops 2148270080 | bytes 12062720 | tf_op jit(solution)/shard_map/dot_general | solution.py:17
  196.8 52.6 %reduce-scatter.2.cloned.1.call-done = f32[1024,256]{1,0:T(8,128)} async-done(((f32[4096,256]{1,0:T(8,128)}), f32[1024,256]{1,0:T(8,128)}) %reduce-scatter.2.cloned.1.call-update) | async-done | bytes 1048592 | tf_op jit(solution)/shard_map/reduce_scatter | solution.py:82
  249.4 1.5 collective-permute-start.5
  250.9 7.3 %fusion.13 = f32[1024,256]{1,0:T(8,128)} fusion(bf16[4096,256]{1,0:T(8,128)(2,1)} %collective-permute-done.1, bf16[1024,4096]{1,0:T(8,128)(2,1)} %copy-done.4), kind=kOutput, calls=%fused_computation.21 | convolution fusion | flops 2147483648 | bytes 11534336 | tf_op jit(solution)/shard_map/dot_general | solution.py:17
  259.5 32.2 %psum.7 = f32[1]{0:T(128)} all-reduce(f32[1]{0:T(128)} %bitcast), channel_id=1, replica_groups=mesh['sys'=2,'col'=4,'seg'=4] {'seg','col'}, use_global_device_ids=true, to_apply=%region_13.14 | all-reduce | flops 1 | bytes 8 | tf_op jit(solution)/shard_map/psum | solution.py:84
  291.7 0.0 copy-start.1
  291.7 0.0 copy-start.2
  291.7 5.9 %fusion.9 = f32[1024,256]{1,0:T(8,128)S(1)} fusion(bf16[4096,256]{1,0:T(8,128)(2,1)S(1)} %collective-permute-done.3, bf16[1024,4096]{1,0:T(8,128)(2,1)} %copy-done.5), kind=kOutput, calls=%fused_computation.17 | convolution fusion | flops 2147483648 | bytes 11534336 | tf_op jit(solution)/shard_map/dot_general | solution.py:17
  297.5 0.0 collective-permute-done.5
  297.5 0.0 copy-done.1
  297.6 0.0 copy-done.2
  297.6 2.6 fusion.23
  (3 shorter events, 0.0 us)
Async XLA Ops:
  7.2 50.4 %all-gather.2.cloned.1.call-start = ((), (), s32[]{:S(2)}) async-start(), calls=%async_computation.1 | async-start | bytes 2621440 | tf_op jit(solution)/shard_map/all_gather | solution.py:41
  7.9 241.5 %reduce-scatter.2.cloned.1.call-start = ((), (), s32[]{:S(2)}) async-start(), calls=%async_computation.2 | async-start | bytes 5242880 | tf_op jit(solution)/shard_map/reduce_scatter | solution.py:82
  57.6 25.5 %collective-permute-start.1 = (bf16[4096,256]{1,0:T(8,128)(2,1)}, bf16[4096,256]{1,0:T(8,128)(2,1)}, u32[]{:S(2)}, u32[]{:S(2)}) collective-permute-start(bf16[4096,256]{1,0:T(8,128)(2,1)} %all-gather.2.cloned.1.call-done), channel_id=1, source_target_pairs={{0,1},{1,2},{2,3},{3,0},{4,5},{5,6},{6,7},{7,4},{8,9},{9,10},{10,1... | collective-permute-start | bytes 6291464 | tf_op jit(solution)/shard_map/ppermute | solution.py:61
  70.6 14.7 %collective-permute-start = (f32[4096]{0:T(1024)S(1)}, f32[4096]{0:T(1024)S(1)}, u32[]{:S(2)}, u32[]{:S(2)}) collective-permute-start(f32[4096]{0:T(1024)S(1)} %all_gather.6), channel_id=1, source_target_pairs={{0,1},{1,2},{2,3},{3,0},{4,5},{5,6},{6,7},{7,4},{8,9},{9,10},{10,1... | collective-permute-start | bytes 49160 | tf_op jit(solution)/shard_map/ppermute | solution.py:62
  85.3 11.1 %copy-start = (bf16[1024,256]{1,0:T(8,128)(2,1)S(1)}, bf16[1024,256]{1,0:T(8,128)(2,1)}, u32[]{:S(2)}) copy-start(bf16[1024,256]{1,0:T(8,128)(2,1)} %param.2) | copy-start | bytes 1572868
  85.3 25.5 %collective-permute-start.3 = (bf16[4096,256]{1,0:T(8,128)(2,1)}, bf16[4096,256]{1,0:T(8,128)(2,1)S(1)}, u32[]{:S(2)}, u32[]{:S(2)}) collective-permute-start(bf16[4096,256]{1,0:T(8,128)(2,1)} %collective-permute-done.1), channel_id=1, source_target_pairs={{0,1},{1,2},{2,3},{3,0},{4,5},{5,6},{6,7},{7,4},{8,9},{9,10},{10,1... | collective-permute-start | bytes 6291464 | tf_op jit(solution)/shard_map/ppermute | solution.py:77
  96.4 8.3 %copy-start.4 = (bf16[1024,4096]{1,0:T(8,128)(2,1)}, bf16[1024,4096]{1,0:T(8,128)(2,1)S(1)}, u32[]{:S(2)}) copy-start(bf16[1024,4096]{1,0:T(8,128)(2,1)S(1)} %get-tuple-element.10) | copy-start | bytes 25165828
  96.4 59.5 %copy-start.3 = (f32[1024]{0:T(1024)S(1)}, f32[1024]{0:T(1024)}, u32[]{:S(2)}) copy-start(f32[1024]{0:T(1024)} %param.3) | copy-start | bytes 12292
  104.7 64.8 %collective-permute-start.4 = (f32[4096,256]{1,0:T(8,128)}, f32[4096,256]{1,0:T(8,128)}, u32[]{:S(2)}, u32[]{:S(2)}) collective-permute-start(f32[4096,256]{1,0:T(8,128)} %fusion.3), channel_id=1, source_target_pairs={{0,1},{1,2},{2,3},{3,0},{4,5},{5,6},{6,7},{7,4},{8,9},{9,10},{10,1... | collective-permute-start | bytes 12582920 | tf_op jit(solution)/shard_map/ppermute | solution.py:79
  106.2 49.7 %collective-permute-start.2 = (f32[4096]{0:T(1024)S(1)}, f32[4096]{0:T(1024)S(1)}, u32[]{:S(2)}, u32[]{:S(2)}) collective-permute-start(f32[4096]{0:T(1024)S(1)} %collective-permute-done), channel_id=1, source_target_pairs={{0,1},{1,2},{2,3},{3,0},{4,5},{5,6},{6,7},{7,4},{8,9},{9,10},{10,1... | collective-permute-start | bytes 49160 | tf_op jit(solution)/shard_map/ppermute | solution.py:78
  166.3 3.2 %copy-start.5 = (bf16[1024,4096]{1,0:T(8,128)(2,1)}, bf16[1024,4096]{1,0:T(8,128)(2,1)S(1)}, u32[]{:S(2)}) copy-start(bf16[1024,4096]{1,0:T(8,128)(2,1)S(1)} %get-tuple-element.11) | copy-start | bytes 25165828
  249.4 48.1 %collective-permute-start.5 = (f32[1024,256]{1,0:T(8,128)}, f32[1024,256]{1,0:T(8,128)}, u32[]{:S(2)}, u32[]{:S(2)}) collective-permute-start(f32[1024,256]{1,0:T(8,128)} %reduce-scatter.2.cloned.1.call-done), channel_id=1, source_target_pairs={{0,2},{1,3},{2,0},{3,1},{4,6},{5,7},{6,4},{7,5},{8,10},{9,11},{10,... | collective-permute-start | bytes 3145736 | tf_op jit(solution)/shard_map/ppermute | solution.py:83
  291.7 5.9 %copy-start.1 = (f32[1024,256]{1,0:T(8,128)S(1)}, f32[1024,256]{1,0:T(8,128)}, u32[]{:S(2)}) copy-start(f32[1024,256]{1,0:T(8,128)} %fusion.15) | copy-start | bytes 3145732
  291.7 5.9 %copy-start.2 = (f32[1024,256]{1,0:T(8,128)S(1)}, f32[1024,256]{1,0:T(8,128)}, u32[]{:S(2)}) copy-start(f32[1024,256]{1,0:T(8,128)} %fusion.13) | copy-start | bytes 3145732
Sparse Core Ops, SparseCore 0:
  9.5 48.0 all-gather.1
  173.7 75.6 reduce-scatter.1
where the time goes:
time: 307 us
  waiting for transfers between devices  163 us (53%)
  matrix products  65.9 us (21%)
  blocking collectives  45.2 us (15%)
  between operations  16.1 us (5%)
  other arithmetic  12.9 us (4%)
  starting transfers between devices  3.45 us (1%)
    reduce_scatter x1, waiting for transfers between devices, per_device(): lax.psum_scatter(reaction, 'col', scatter_dimension=0, tiled=True)  52.6 us
    all_gather x1, waiting for transfers between devices, per_device(): x_team = lax.all_gather(x_own, 'col', axis=0, tiled=True)  49.7 us
    ppermute x1, waiting for transfers between devices, per_device(): q_vis = lax.ppermute(q_vis, 'seg', forward)  44.5 us
    dot_general x3, matrix products, pair_weights(): lax.dot_general(x_host, x_vis, (((1,), (1,)), ((), ())), preferred_elemen...  34.5 us
    psum x1, blocking collectives, per_device(): energy = lax.psum(energy, ('seg', 'col'))  32.2 us
    dot_general x3, matrix products, host_terms(): pulled = jnp.dot(w_low, x_vis, preferred_element_type=jnp.float32)  20.5 us
    all_gather x1, blocking collectives, per_device(): q_team = lax.all_gather(q_own, 'col', axis=0, tiled=True)  13 us
    ppermute x1, waiting for transfers between devices, per_device(): x_vis = lax.ppermute(x_team, 'seg', forward)  11.2 us
  transfers between devices with their start and end apart: 8, of which 5 were waited for; matrix products, arithmetic and copies ran while one was open for 24% of the time, Pallas kernels for 0%

commit v1 on v0

v1 whole, which is shorter than its diff:
```python
import functools
import math

import jax
import jax.numpy as jnp
from jax import lax
from jax.experimental import pallas as pl
from jax.experimental.pallas import tpu as pltpu
from jax.sharding import PartitionSpec as P

ROW_AXES = ('sys', 'seg', 'col')
MESH = pl.DeviceIdType.MESH
NT = (((1,), (1,)), ((), ()))
PARTS = 4
LANES = 128


def pair_kernel(x_hbm, q_ref, out_ref, e_ref, xs, aq, es, a_col, q_col, force, row_sum,
                load_sem, recv_sem, aq_recv, e_recv, send_sem, aq_send, e_send):
    rows, feat = x_hbm.shape
    part = rows // PARTS
    groups = rows // LANES
    scale = 0.5 * math.log2(math.e) / feat
    z = lax.axis_index('col')
    seg = lax.axis_index('seg')
    y, c = seg // 2, seg % 2
    corner = (z == 0) | (z == 3)
    near = 1 + z % 2
    far = 3 * (1 - z // 2)
    other = 6 - z - near - far
    plane = (1 - 2 * c) * 4 * PARTS

    def line(e):
        return jnp.where(e == 0, near, jnp.where(e == 1, other, far))

    def chunk(yy, zz, k):
        return ((2 * yy + c) * 4 + zz) * PARTS + k

    def block_of(ch):
        return ch // PARTS

    own = chunk(y, z, 0)
    DOWN, UP, SIDE, TWIN = range(4)
    device = [{'col': z - 1}, {'col': z + 1}, {'seg': 2 * (1 - y) + c}, {'seg': 2 * y + 1 - c}]

    def send(way, ch):
        pltpu.make_async_remote_copy(
            src_ref=xs.at[ch], dst_ref=xs.at[ch], send_sem=send_sem.at[way], recv_sem=recv_sem.at[ch],
            device_id=device[way], device_id_type=MESH).start()

    def send_if(cond, way, ch):
        @pl.when(cond)
        def _():
            send(way, ch)

    def arrive(ch):
        pltpu.make_async_copy(xs.at[ch], xs.at[ch], recv_sem.at[ch]).wait()

    def onward(zb, ch):
        send_if((zb > z) & (z > 0), DOWN, ch)
        send_if((zb < z) & (z < 3), UP, ch)

    def line_event(zb, k):
        ch = chunk(y, zb, k)
        arrive(ch)
        onward(zb, ch)
        send_if((k < PARTS - 1) | (zb - z == 3) | (z - zb == 3), SIDE, ch)
        send(TWIN, ch)

    def aq_copy(blk, dev, sem):
        return pltpu.make_async_remote_copy(
            src_ref=aq.at[blk], dst_ref=aq.at[blk], send_sem=sem, recv_sem=aq_recv.at[blk],
            device_id=dev, device_id_type=MESH)

    def aq_arrive(blk):
        pltpu.make_async_copy(aq.at[blk], aq.at[blk], aq_recv.at[blk]).wait()

    def aq_event(yy, zz):
        blk = block_of(chunk(yy, zz, 0))
        aq_arrive(blk)
        aq_copy(blk, device[TWIN], aq_send.at[1]).start()
        aq_arrive(blk + plane // PARTS)

    loads = [pltpu.make_async_copy(x_hbm.at[pl.ds(k * part, part)], xs.at[own + k], load_sem.at[k])
             for k in range(PARTS)]
    for load in loads:
        load.start()
    barrier = pltpu.get_barrier_semaphore()
    place = seg * 4 + z
    for d in range(1, 16):
        peer = (place + d) % 16
        pl.semaphore_signal(barrier, inc=1, device_id={'seg': peer // 4, 'col': peer % 4}, device_id_type=MESH)
    pl.semaphore_wait(barrier, 15)

    def send_own(k):
        send_if(z > 0, DOWN, own + k)
        send_if(z < 3, UP, own + k)
        send(SIDE, own + k)
        send(TWIN, own + k)

    for k in range(PARTS):
        loads[k].wait()
        if k < 2:
            send_own(k)

    for k in range(PARTS):
        wide = xs[own + k].astype(jnp.float32)
        a_col[pl.ds(k * part, part), :] = jnp.broadcast_to(
            scale * jnp.sum(wide * wide, axis=1, keepdims=True), (part, LANES))
    own_blk = block_of(own)
    for g in range(groups):
        span = pl.ds(g * LANES, LANES)
        aq[own_blk, g:g + 1, :] = jnp.transpose(a_col[span, :])[0:1, :]
        aq[own_blk, groups + g:groups + g + 1, :] = q_ref[g:g + 1, :]
        q_col[span, :] = jnp.transpose(jnp.broadcast_to(q_ref[g:g + 1, :], (LANES, LANES)))
    force[...] = jnp.zeros_like(force)
    row_sum[...] = jnp.zeros_like(row_sum)
    aq_copy(own_blk, device[TWIN], aq_send.at[1]).start()
    for d in range(1, 8):
        peer = (y * 4 + z + d) % 8
        aq_copy(own_blk, {'seg': 2 * (peer // 4) + c, 'col': peer % 4}, aq_send.at[0]).start()
    for k in range(2, PARTS):
        send_own(k)

    def tile(r, chunks, parts_of, masked):
        span = pl.ds(r * part, part)
        acc = force[span, :]
        total = row_sum[span, :]
        a_i = jnp.concatenate([a_col[span, :]] * 2, axis=1)
        q_i = jnp.concatenate([q_col[span, :]] * 2, axis=1)
        x_i = xs[own + r]
        for n, (ch, k) in enumerate(zip(chunks, parts_of)):
            x_j = xs[ch]
            blk = block_of(ch)
            def lanes(first):
                return jnp.concatenate([aq[blk, pl.ds(first + h, 1), :] for h in range(2)], axis=1)
            dots = lax.dot_general(x_i, x_j, NT, preferred_element_type=jnp.float32)
            power = jnp.minimum((2.0 * scale * dots - lanes(2 * k)) - a_i, 0.0)
            weights = (q_i * lanes(groups + 2 * k)) * jnp.exp2(power)
            if masked and n == r:
                rid = lax.broadcasted_iota(jnp.int32, weights.shape, 0)
                cid = lax.broadcasted_iota(jnp.int32, weights.shape, 1)
                weights = jnp.where(rid == cid, 0.0, weights)
            total = total + (weights[:, :LANES] + weights[:, LANES:])
            acc = acc + jnp.dot(weights.astype(jnp.bfloat16), x_j, preferred_element_type=jnp.float32)
        force[span, :] = acc
        row_sum[span, :] = total

    def pairs(chunks, parts_of, masked=False):
        for r in range(PARTS):
            tile(r, chunks, parts_of, masked)

    pairs([own + k for k in range(PARTS)], range(PARTS), masked=True)
    aq_arrive(own_blk + plane // PARTS)
    for k in range(PARTS):
        arrive(own + plane + k)
    pairs([own + plane + k for k in range(PARTS)], range(PARTS))

    LAST = PARTS - 1

    def step(u, carry):
        k4 = u % 4
        @pl.when(corner & (u < 12))
        def _():
            line_event(line(u // 4), k4)

        @pl.when(corner & (u >= 12))
        def _():
            ch = chunk(1 - y, line(u - 12), LAST)
            arrive(ch)
            send(TWIN, ch)

        @pl.when(~corner & (u < 4))
        def _():
            line_event(near, k4)
            line_event(other, k4)

        @pl.when(~corner & (u >= 4) & (u < 8))
        def _():
            line_event(far, k4)

        @pl.when(~corner & (u == 7))
        def _():
            ch = chunk(1 - y, z, LAST)
            send_if(z == 1, DOWN, ch)
            send_if(z == 2, UP, ch)

        @pl.when(~corner & (u >= 8) & (u < 11))
        def _():
            zb = line(u - 8)
            ch = chunk(1 - y, zb, LAST)
            arrive(ch)
            @pl.when(u < 10)
            def _():
                onward(zb, ch)
            send(TWIN, ch)

        side_zb = jnp.where(u < 4, z, jnp.where(u < 13, line((u - 4 + 3 * 4) // 3 - 4), far))
        side_k = jnp.where(u < 4, u, jnp.where(u < 13, (u - 4 + 3 * 4) % 3, LAST))
        side = chunk(1 - y, side_zb, side_k)

        @pl.when(corner | (u < 13))
        def _():
            arrive(side)
            send(TWIN, side)

        @pl.when(u == 3)
        def _():
            send_if(z < 2, UP, side)
            send_if(z >= 2, DOWN, side)

        for when, events in ((0, ((y, near), (1 - y, z))), (4, ((y, other), (1 - y, near))),
                             (7, ((1 - y, other),)), (8, ((y, far),)), (10, ((1 - y, far),))):
            @pl.when(u == when)
            def _():
                for yy, zz in events:
                    aq_event(yy, zz)

        along_y = jnp.where(u < 12, y, 1 - y)
        along_z = jnp.where(u < 12, line(u // 4), line(u - 12))
        along_k = jnp.where(u < 12, k4, LAST)
        along = chunk(along_y, along_z, along_k)
        arrive(along + plane)
        arrive(side + plane)
        pairs([along, side, along + plane, side + plane], [along_k, side_k, along_k, side_k])
        return carry

    lax.fori_loop(0, 14, step, 0)

    tile_sum = jnp.sum(row_sum[...].reshape(rows // 8, 8, LANES), axis=0)
    es[place] = tile_sum
    def e_copy(peer):
        return pltpu.make_async_remote_copy(
            src_ref=es.at[place], dst_ref=es.at[place], send_sem=e_send, recv_sem=e_recv,
            device_id={'seg': peer // 4, 'col': peer % 4}, device_id_type=MESH)
    for d in range(1, 16):
        e_copy((place + d) % 16).start()

    inv_len2 = 1.0 / feat
    for r in range(PARTS):
        span = pl.ds(r * part, part)
        full = jnp.sum(row_sum[span, :], axis=1, keepdims=True)
        out_ref[span, :] = (full * xs[own + r].astype(jnp.float32) - force[span, :]) * inv_len2

    def drain(sem, ref):
        pltpu.make_async_copy(ref, ref, sem).wait()

    drain(send_sem.at[TWIN], xs.at[pl.ds(0, 8 * PARTS)])
    drain(aq_send.at[0], aq.at[pl.ds(0, 7)])
    drain(aq_send.at[1], aq.at[pl.ds(0, 8)])
    for zz, counts in enumerate(((0, 5, 14), (14, 10, 13), (10, 14, 13), (5, 0, 14))):
        @pl.when(z == zz)
        def _():
            for way, count in zip((DOWN, UP, SIDE), counts):
                if count:
                    drain(send_sem.at[way], xs.at[pl.ds(0, count)])
    drain(e_recv, es.at[pl.ds(0, 15)])
    drain(e_send, es.at[pl.ds(0, 15)])
    e_ref[0] = 0.5 * jnp.sum(es[...])


def solution(mesh):
    assert (mesh.shape['seg'], mesh.shape['col']) == (4, 4)

    def per_device(x_own, q_own):
        rows, feat = x_own.shape
        part = rows // PARTS
        groups = rows // LANES
        f32, bf16 = jnp.float32, jnp.bfloat16
        vmem = pltpu.VMEM
        dma = pltpu.SemaphoreType.DMA
        return pl.pallas_call(
            pair_kernel,
            out_shape=(jax.ShapeDtypeStruct((rows, feat), f32), jax.ShapeDtypeStruct((1,), f32)),
            in_specs=[pl.BlockSpec(memory_space=pl.ANY), pl.BlockSpec(memory_space=vmem)],
            out_specs=(pl.BlockSpec(memory_space=vmem), pl.BlockSpec(memory_space=pltpu.SMEM)),
            scratch_shapes=[
                vmem((16 * PARTS, part, feat), bf16), vmem((16, 2 * groups, LANES), f32), vmem((16, 8, LANES), f32),
                vmem((rows, LANES), f32), vmem((rows, LANES), f32), vmem((rows, feat), f32), vmem((rows, LANES), f32),
                dma((PARTS,)), dma((16 * PARTS,)), dma((16,)), dma, dma((4,)), dma((2,)), dma],
            compiler_params=pltpu.CompilerParams(
                collective_id=0, has_side_effects=True, vmem_limit_bytes=40 * 2 ** 20),
        )(x_own, q_own.reshape(groups, LANES))

    row_spec = P(ROW_AXES, None)
    return jax.shard_map(per_device, mesh=mesh, in_specs=(row_spec, P(ROW_AXES)),
                         out_specs=(row_spec, P('sys')), check_vma=False)
```

time: 307 us -> 70.4 us (0.23)
  waiting for transfers between devices: 163 us -> 0 us
  matrix products: 65.9 us -> 0 us
  Pallas kernels: 0 us -> 65.1 us
  blocking collectives: 45.2 us -> 0 us
  between operations: 16.1 us -> 2.41 us
  other arithmetic: 12.9 us -> 0 us
  starting transfers between devices: 3.45 us -> 0 us
    dot_general x8 -> x0, matrix products: 65.9 us -> none  [the longest x3 34.5 us: pair_weights(): lax.dot_general(x_host, x_vis, (((1,), (1,)), ((), ())), preferred_elemen...]
    pallas_call x0 -> x1, Pallas kernels: none -> 65.1 us  [per_device(): pl.pallas_call(pair_kernel, out_shape=(jax.ShapeDtypeStruct((rows, feat),...]
    ppermute x6 -> x0, waiting for transfers between devices: 59.9 us -> none  [the longest x1 44.5 us: per_device(): q_vis = lax.ppermute(q_vis, 'seg', forward)]
    reduce_scatter x1 -> x0, waiting for transfers between devices: 52.6 us -> none  [per_device(): lax.psum_scatter(reaction, 'col', scatter_dimension=0, tiled=True)]
    all_gather x1 -> x0, waiting for transfers between devices: 49.7 us -> none  [per_device(): x_team = lax.all_gather(x_own, 'col', axis=0, tiled=True)]
    psum x1 -> x0, blocking collectives: 32.2 us -> none  [per_device(): energy = lax.psum(energy, ('seg', 'col'))]
    all_gather x1 -> x0, blocking collectives: 13 us -> none  [per_device(): q_team = lax.all_gather(q_own, 'col', axis=0, tiled=True)]
    reduce_sum x4 -> x0, other arithmetic: 6.28 us -> none  [the longest x3 5.03 us: pair_weights(): sq_vis = jnp.sum(jnp.square(x_vis.astype(jnp.float32)), axis=1)]
  transfers between devices with their start and end apart: 8 -> 0, of which waited for: 5 -> 0; matrix products, arithmetic and copies ran while one was open for 24% -> 0% of each run, Pallas kernels for 0% -> 0%
where the time goes in v1:
time: 70.4 us; the launch traced here: 70.2 us
  Pallas kernels  65.1 us (92%)
  local copies, waits for them, and re-layouts  2.69 us (4%)
  between operations  2.41 us (3%)
    pallas_call x1, Pallas kernels, per_device(): pl.pallas_call(pair_kernel, out_shape=(jax.ShapeDtypeStruct((rows, feat),...  65.1 us
    unnamed x5, local copies, waits for them, and re-layouts  2.69 us

profile of v1, /device:TPU:0, one launch (start us, length us, event | category | flops | bytes accessed | tf_op | source)
XLA Modules:
  0.0 70.2 jit_solution(968281102588506328)
XLA Ops:
  0.6 0.0 copy-start
  0.6 1.0 %copy-done = bf16[1024,256]{1,0:T(8,128)(2,1)S(1)} copy-done((bf16[1024,256]{1,0:T(8,128)(2,1)S(1)}, bf16[1024,256]{1,0:T(8,128)(2,1)}, u32[]{:S(2)}) %copy-start) | copy-done | bytes 524312
  1.7 0.0 copy-start.1
  1.7 0.7 copy-done.1
  2.4 65.1 %shard_map.41 = (f32[1024,256]{1,0:T(8,128)S(1)}, f32[1]{0:T(128)}) custom-call(bf16[1024,256]{1,0:T(8,128)(2,1)S(1)} %copy-done, f32[8,128]{1,0:T(8,128)S(1)} %bitcast.1), custom_call_target="tpu_custom_call" | custom-call | tf_op jit(solution)/shard_map/pallas_call | solution.py:272
  67.5 1.0 %copy.6 = f32[1024,256]{1,0:T(8,128)} copy(f32[1024,256]{1,0:T(8,128)S(1)} %get-tuple-element.4) | data formatting | bytes 2097152
Async XLA Ops:
  0.6 1.0 %copy-start = (bf16[1024,256]{1,0:T(8,128)(2,1)S(1)}, bf16[1024,256]{1,0:T(8,128)(2,1)}, u32[]{:S(2)}) copy-start(bf16[1024,256]{1,0:T(8,128)(2,1)} %x_hbm.1) | copy-start | bytes 1572868
  1.7 0.7 copy-start.1

commit v2 on v1

--- a/solution.py
+++ b/solution.py
@@ -15,7 +15,7 @@
 LANES = 128
 
 
-def pair_kernel(x_hbm, q_ref, out_ref, e_ref, xs, aq, es, a_col, q_col, force, row_sum,
+def pair_kernel(x_hbm, q_hbm, out_ref, e_ref, xs, aq, es, q_ref, a_col, q_col, force, row_sum,
                 load_sem, recv_sem, aq_recv, e_recv, send_sem, aq_send, e_send):
     rows, feat = x_hbm.shape
     part = rows // PARTS
@@ -60,6 +60,19 @@
         send_if((zb > z) & (z > 0), DOWN, ch)
         send_if((zb < z) & (z < 3), UP, ch)
 
+    def aq_send_to(way, blk):
+        pltpu.make_async_remote_copy(
+            src_ref=aq.at[blk], dst_ref=aq.at[blk], send_sem=aq_send.at[way], recv_sem=aq_recv.at[blk],
+            device_id=device[way], device_id_type=MESH).start()
+
+    def aq_send_if(cond, way, blk):
+        @pl.when(cond)
+        def _():
+            aq_send_to(way, blk)
+
+    def aq_arrive(blk):
+        pltpu.make_async_copy(aq.at[blk], aq.at[blk], aq_recv.at[blk]).wait()
+
     def line_event(zb, k):
         ch = chunk(y, zb, k)
         arrive(ch)
@@ -67,60 +80,56 @@
         send_if((k < PARTS - 1) | (zb - z == 3) | (z - zb == 3), SIDE, ch)
         send(TWIN, ch)
 
-    def aq_copy(blk, dev, sem):
-        return pltpu.make_async_remote_copy(
-            src_ref=aq.at[blk], dst_ref=aq.at[blk], send_sem=sem, recv_sem=aq_recv.at[blk],
-            device_id=dev, device_id_type=MESH)
-
-    def aq_arrive(blk):
-        pltpu.make_async_copy(aq.at[blk], aq.at[blk], aq_recv.at[blk]).wait()
-
-    def aq_event(yy, zz):
-        blk = block_of(chunk(yy, zz, 0))
-        aq_arrive(blk)
-        aq_copy(blk, device[TWIN], aq_send.at[1]).start()
-        aq_arrive(blk + plane // PARTS)
+        @pl.when(k == 0)
+        def _():
+            blk = block_of(ch)
+            aq_arrive(blk)
+            aq_send_if((zb > z) & (z > 0), DOWN, blk)
+            aq_send_if((zb < z) & (z < 3), UP, blk)
+            aq_send_to(SIDE, blk)
+            aq_send_to(TWIN, blk)
 
     loads = [pltpu.make_async_copy(x_hbm.at[pl.ds(k * part, part)], xs.at[own + k], load_sem.at[k])
              for k in range(PARTS)]
+    loads.append(pltpu.make_async_copy(q_hbm, q_ref, load_sem.at[PARTS]))
     for load in loads:
         load.start()
     barrier = pltpu.get_barrier_semaphore()
-    place = seg * 4 + z
-    for d in range(1, 16):
-        peer = (place + d) % 16
-        pl.semaphore_signal(barrier, inc=1, device_id={'seg': peer // 4, 'col': peer % 4}, device_id_type=MESH)
-    pl.semaphore_wait(barrier, 15)
-
-    def send_own(k):
-        send_if(z > 0, DOWN, own + k)
-        send_if(z < 3, UP, own + k)
-        send(SIDE, own + k)
-        send(TWIN, own + k)
-
+
+    def greet(way):
+        pl.semaphore_signal(barrier, inc=1, device_id=device[way], device_id_type=MESH)
+
+    pl.when(z > 0)(lambda: greet(DOWN))
+    pl.when(z < 3)(lambda: greet(UP))
+    greet(SIDE)
+    greet(TWIN)
+
+    own_blk = block_of(own)
+    loads[PARTS].wait()
     for k in range(PARTS):
         loads[k].wait()
-        if k < 2:
-            send_own(k)
-
-    for k in range(PARTS):
         wide = xs[own + k].astype(jnp.float32)
         a_col[pl.ds(k * part, part), :] = jnp.broadcast_to(
             scale * jnp.sum(wide * wide, axis=1, keepdims=True), (part, LANES))
-    own_blk = block_of(own)
     for g in range(groups):
         span = pl.ds(g * LANES, LANES)
         aq[own_blk, g:g + 1, :] = jnp.transpose(a_col[span, :])[0:1, :]
         aq[own_blk, groups + g:groups + g + 1, :] = q_ref[g:g + 1, :]
         q_col[span, :] = jnp.transpose(jnp.broadcast_to(q_ref[g:g + 1, :], (LANES, LANES)))
+
+    pl.semaphore_wait(barrier, jnp.where(corner, 3, 4))
+    for k in range(PARTS):
+        send_if(z > 0, DOWN, own + k)
+        send_if(z < 3, UP, own + k)
+        send(SIDE, own + k)
+        send(TWIN, own + k)
+        if k == 0:
+            aq_send_if(z > 0, DOWN, own_blk)
+            aq_send_if(z < 3, UP, own_blk)
+            aq_send_to(SIDE, own_blk)
+            aq_send_to(TWIN, own_blk)
     force[...] = jnp.zeros_like(force)
     row_sum[...] = jnp.zeros_like(row_sum)
-    aq_copy(own_blk, device[TWIN], aq_send.at[1]).start()
-    for d in range(1, 8):
-        peer = (y * 4 + z + d) % 8
-        aq_copy(own_blk, {'seg': 2 * (peer // 4) + c, 'col': peer % 4}, aq_send.at[0]).start()
-    for k in range(2, PARTS):
-        send_own(k)
 
     def tile(r, chunks, parts_of, masked):
         span = pl.ds(r * part, part)
@@ -154,7 +163,7 @@
     aq_arrive(own_blk + plane // PARTS)
     for k in range(PARTS):
         arrive(own + plane + k)
-    pairs([own + plane + k for k in range(PARTS)], range(PARTS))
+    pairs([own + plane + k for k in range(2)], range(2))
 
     LAST = PARTS - 1
 
@@ -209,24 +218,43 @@
             send_if(z < 2, UP, side)
             send_if(z >= 2, DOWN, side)
 
-        for when, events in ((0, ((y, near), (1 - y, z))), (4, ((y, other), (1 - y, near))),
-                             (7, ((1 - y, other),)), (8, ((y, far),)), (10, ((1 - y, far),))):
-            @pl.when(u == when)
-            def _():
-                for yy, zz in events:
-                    aq_event(yy, zz)
-
-        along_y = jnp.where(u < 12, y, 1 - y)
-        along_z = jnp.where(u < 12, line(u // 4), line(u - 12))
-        along_k = jnp.where(u < 12, k4, LAST)
-        along = chunk(along_y, along_z, along_k)
-        arrive(along + plane)
-        arrive(side + plane)
-        pairs([along, side, along + plane, side + plane], [along_k, side_k, along_k, side_k])
-        return carry
-
-    lax.fori_loop(0, 14, step, 0)
-
+        @pl.when((u == 0) | (u == 4) | (u == 7) | (u == 10))
+        def _():
+            blk = block_of(side)
+            aq_arrive(blk)
+            aq_send_to(TWIN, blk)
+
+        along = jnp.where(u < 12, chunk(y, line(u // 4), k4), chunk(1 - y, line(u - 12), LAST))
+        pairs_of_step(u, along, side, carry)
+        return along, side
+
+    def from_twin(u, along, side):
+        @pl.when((u == 0) | (u == 4) | (u == 8))
+        def _():
+            aq_arrive(block_of(along))
+
+        @pl.when((u == 0) | (u == 4) | (u == 7) | (u == 10))
+        def _():
+            aq_arrive(block_of(side))
+
+        arrive(along)
+        arrive(side)
+
+    def pairs_of_step(u, along, side, before):
+        along_before, side_before = (ch + plane for ch in before)
+
+        @pl.when(u > 0)
+        def _():
+            from_twin(u - 1, along_before, side_before)
+
+        chunks = [along, side, along_before, side_before]
+        pairs(chunks, [ch % PARTS for ch in chunks])
+
+    along, side = lax.fori_loop(0, 14, step, (own + 2, own + 3))
+    from_twin(13, along + plane, side + plane)
+    pairs([along + plane, side + plane], [along % PARTS, side % PARTS])
+
+    place = seg * 4 + z
     tile_sum = jnp.sum(row_sum[...].reshape(rows // 8, 8, LANES), axis=0)
     es[place] = tile_sum
     def e_copy(peer):
@@ -246,14 +274,18 @@
         pltpu.make_async_copy(ref, ref, sem).wait()
 
     drain(send_sem.at[TWIN], xs.at[pl.ds(0, 8 * PARTS)])
-    drain(aq_send.at[0], aq.at[pl.ds(0, 7)])
-    drain(aq_send.at[1], aq.at[pl.ds(0, 8)])
+    drain(aq_send.at[TWIN], aq.at[pl.ds(0, 8)])
+    drain(aq_send.at[SIDE], aq.at[pl.ds(0, 4)])
     for zz, counts in enumerate(((0, 5, 14), (14, 10, 13), (10, 14, 13), (5, 0, 14))):
         @pl.when(z == zz)
         def _():
             for way, count in zip((DOWN, UP, SIDE), counts):
                 if count:
                     drain(send_sem.at[way], xs.at[pl.ds(0, count)])
+            if zz:
+                drain(aq_send.at[DOWN], aq.at[pl.ds(0, 4 - zz)])
+            if zz < 3:
+                drain(aq_send.at[UP], aq.at[pl.ds(0, zz + 1)])
     drain(e_recv, es.at[pl.ds(0, 15)])
     drain(e_send, es.at[pl.ds(0, 15)])
     e_ref[0] = 0.5 * jnp.sum(es[...])
@@ -272,12 +304,13 @@
         return pl.pallas_call(
             pair_kernel,
             out_shape=(jax.ShapeDtypeStruct((rows, feat), f32), jax.ShapeDtypeStruct((1,), f32)),
-            in_specs=[pl.BlockSpec(memory_space=pl.ANY), pl.BlockSpec(memory_space=vmem)],
+            in_specs=[pl.BlockSpec(memory_space=pltpu.HBM)] * 2,
             out_specs=(pl.BlockSpec(memory_space=vmem), pl.BlockSpec(memory_space=pltpu.SMEM)),
             scratch_shapes=[
                 vmem((16 * PARTS, part, feat), bf16), vmem((16, 2 * groups, LANES), f32), vmem((16, 8, LANES), f32),
+                vmem((groups, LANES), f32),
                 vmem((rows, LANES), f32), vmem((rows, LANES), f32), vmem((rows, feat), f32), vmem((rows, LANES), f32),
-                dma((PARTS,)), dma((16 * PARTS,)), dma((16,)), dma, dma((4,)), dma((2,)), dma],
+                dma((PARTS + 1,)), dma((16 * PARTS,)), dma((16,)), dma, dma((4,)), dma((4,)), dma],
             compiler_params=pltpu.CompilerParams(
                 collective_id=0, has_side_effects=True, vmem_limit_bytes=40 * 2 ** 20),
         )(x_own, q_own.reshape(groups, LANES))

time: 70.4 us -> 61.5 us (0.87)
  Pallas kernels: 65.1 us -> 56.2 us
    pallas_call x1, Pallas kernels: 65.1 us -> 56.2 us  [per_device(): pl.pallas_call(pair_kernel, out_shape=(jax.ShapeDtypeStruct((rows, feat),...]
where the time goes in v2:
time: 61.5 us; the launch traced here: 61.3 us
  Pallas kernels  56.2 us (91%)
  local copies, waits for them, and re-layouts  2.69 us (4%)
  between operations  2.41 us (4%)
    pallas_call x1, Pallas kernels, per_device(): pl.pallas_call(pair_kernel, out_shape=(jax.ShapeDtypeStruct((rows, feat),...  56.2 us
    unnamed x5, local copies, waits for them, and re-layouts  2.69 us

profile of v2, /device:TPU:0, one launch (start us, length us, event | category | flops | bytes accessed | tf_op | source)
XLA Modules:
  0.0 61.3 jit_solution(4924985046347782806)
XLA Ops:
  0.6 0.0 copy-start
  0.6 1.0 %copy-done = bf16[1024,256]{1,0:T(8,128)(2,1)S(1)} copy-done((bf16[1024,256]{1,0:T(8,128)(2,1)S(1)}, bf16[1024,256]{1,0:T(8,128)(2,1)}, u32[]{:S(2)}) %copy-start) | copy-done | bytes 524312
  1.7 0.0 copy-start.1
  1.7 0.7 %copy-done.1 = f32[1024]{0:T(1024)S(1)} copy-done((f32[1024]{0:T(1024)S(1)}, f32[1024]{0:T(1024)}, u32[]{:S(2)}) %copy-start.1) | copy-done | bytes 4120
  2.4 56.2 %shard_map.41 = (f32[1024,256]{1,0:T(8,128)S(1)}, f32[1]{0:T(128)}) custom-call(bf16[1024,256]{1,0:T(8,128)(2,1)S(1)} %copy-done, f32[8,128]{1,0:T(8,128)S(1)} %bitcast.1), custom_call_target="tpu_custom_call" | custom-call | tf_op jit(solution)/shard_map/pallas_call | solution.py:304
  58.6 1.0 %copy.6 = f32[1024,256]{1,0:T(8,128)} copy(f32[1024,256]{1,0:T(8,128)S(1)} %get-tuple-element.4) | data formatting | bytes 2097152
Async XLA Ops:
  0.6 1.0 %copy-start = (bf16[1024,256]{1,0:T(8,128)(2,1)S(1)}, bf16[1024,256]{1,0:T(8,128)(2,1)}, u32[]{:S(2)}) copy-start(bf16[1024,256]{1,0:T(8,128)(2,1)} %x_hbm.1) | copy-start | bytes 1572868
  1.7 0.7 %copy-start.1 = (f32[1024]{0:T(1024)S(1)}, f32[1024]{0:T(1024)}, u32[]{:S(2)}) copy-start(f32[1024]{0:T(1024)} %param.3) | copy-start | bytes 12292

commit v3 on v2

--- a/solution.py
+++ b/solution.py
@@ -15,7 +15,8 @@
 LANES = 128
 
 
-def pair_kernel(x_hbm, q_hbm, out_ref, e_ref, xs, aq, es, q_ref, a_col, q_col, force, row_sum,
+def pair_kernel(x_hbm, q_hbm, out_ref, e_ref, xs, aq, es, e_acc, q_ref, a_col, q_col,
+                a_end, q_end, force, row_sum,
                 load_sem, recv_sem, aq_recv, e_recv, send_sem, aq_send, e_send):
     rows, feat = x_hbm.shape
     part = rows // PARTS
@@ -40,6 +41,7 @@
         return ch // PARTS
 
     own = chunk(y, z, 0)
+    LAST = PARTS - 1
     DOWN, UP, SIDE, TWIN = range(4)
     device = [{'col': z - 1}, {'col': z + 1}, {'seg': 2 * (1 - y) + c}, {'seg': 2 * y + 1 - c}]
 
@@ -77,7 +79,8 @@
         ch = chunk(y, zb, k)
         arrive(ch)
         onward(zb, ch)
-        send_if((k < PARTS - 1) | (zb - z == 3) | (z - zb == 3), SIDE, ch)
+        near_side = jnp.where((zb == near) | (corner & (zb == other)), 3, 2)
+        send_if(k < jnp.where(corner & (zb == far), PARTS, near_side), SIDE, ch)
         send(TWIN, ch)
 
         @pl.when(k == 0)
@@ -130,34 +133,70 @@
             aq_send_to(TWIN, own_blk)
     force[...] = jnp.zeros_like(force)
     row_sum[...] = jnp.zeros_like(row_sum)
+    e_acc[...] = jnp.zeros_like(e_acc)
+
+    def share(ch):
+        same_line = (block_of(ch) // 8) == y
+        z_j = block_of(ch) % 4
+        at_corner = jnp.where((z_j == z) | ((z_j == far) & same_line), 0.5, 0.0)
+        at_middle = jnp.where((z_j == 1) | (z_j == 2), 0.5, 1.0)
+        return jnp.where(corner, at_corner, at_middle)
+
+    def weights_of(x_i, a_i, q_i, ch, k):
+        blk = block_of(ch)
+        def lanes(first):
+            return jnp.concatenate([aq[blk, pl.ds(first + h, 1), :] for h in range(2)], axis=1)
+        a_i, q_i = (jnp.concatenate([v] * 2, axis=1) for v in (a_i, q_i))
+        dots = lax.dot_general(x_i, xs[ch], NT, preferred_element_type=jnp.float32)
+        power = jnp.minimum((2.0 * scale * dots - lanes(2 * k)) - a_i, 0.0)
+        return (q_i * lanes(groups + 2 * k)) * jnp.exp2(power)
+
+    def fold(weights):
+        return weights[:, :LANES] + weights[:, LANES:]
+
+    def stack(halves):
+        return jnp.sum(halves.reshape(part // 8, 8, LANES), axis=0)
 
     def tile(r, chunks, parts_of, masked):
         span = pl.ds(r * part, part)
         acc = force[span, :]
         total = row_sum[span, :]
-        a_i = jnp.concatenate([a_col[span, :]] * 2, axis=1)
-        q_i = jnp.concatenate([q_col[span, :]] * 2, axis=1)
-        x_i = xs[own + r]
+        e_part = jnp.zeros((8, LANES), jnp.float32)
         for n, (ch, k) in enumerate(zip(chunks, parts_of)):
-            x_j = xs[ch]
-            blk = block_of(ch)
-            def lanes(first):
-                return jnp.concatenate([aq[blk, pl.ds(first + h, 1), :] for h in range(2)], axis=1)
-            dots = lax.dot_general(x_i, x_j, NT, preferred_element_type=jnp.float32)
-            power = jnp.minimum((2.0 * scale * dots - lanes(2 * k)) - a_i, 0.0)
-            weights = (q_i * lanes(groups + 2 * k)) * jnp.exp2(power)
+            weights = weights_of(xs[own + r], a_col[span, :], q_col[span, :], ch, k)
             if masked and n == r:
                 rid = lax.broadcasted_iota(jnp.int32, weights.shape, 0)
                 cid = lax.broadcasted_iota(jnp.int32, weights.shape, 1)
                 weights = jnp.where(rid == cid, 0.0, weights)
-            total = total + (weights[:, :LANES] + weights[:, LANES:])
-            acc = acc + jnp.dot(weights.astype(jnp.bfloat16), x_j, preferred_element_type=jnp.float32)
+            halves = fold(weights)
+            total = total + halves
+            e_part = e_part + share(ch) * stack(halves)
+            acc = acc + jnp.dot(weights.astype(jnp.bfloat16), xs[ch], preferred_element_type=jnp.float32)
         force[span, :] = acc
         row_sum[span, :] = total
+        e_acc[...] += e_part
 
     def pairs(chunks, parts_of, masked=False):
         for r in range(PARTS):
             tile(r, chunks, parts_of, masked)
+
+    end_rows = chunk(y, 0, 0)
+    end_cols = ((2 * (1 - y) + z - 1) * 4 + 3) * PARTS
+
+    def end_vectors():
+        blk = block_of(end_rows)
+        for g in range(groups):
+            for ref, first in ((a_end, 0), (q_end, groups)):
+                row = aq[blk, first + g:first + g + 1, :]
+                ref[pl.ds(g * LANES, LANES), :] = jnp.transpose(jnp.broadcast_to(row, (LANES, LANES)))
+
+    def end_energy(k):
+        e_part = jnp.zeros((8, LANES), jnp.float32)
+        for r in range(PARTS):
+            span = pl.ds(r * part, part)
+            e_part = e_part + stack(fold(weights_of(
+                xs[end_rows + r], a_end[span, :], q_end[span, :], end_cols + k, k)))
+        e_acc[...] += e_part
 
     pairs([own + k for k in range(PARTS)], range(PARTS), masked=True)
     aq_arrive(own_blk + plane // PARTS)
@@ -165,28 +204,87 @@
         arrive(own + plane + k)
     pairs([own + plane + k for k in range(2)], range(2))
 
-    LAST = PARTS - 1
+    place = seg * 4 + z
+
+    def send_energy():
+        for d in range(1, 16):
+            peer = (place + d) % 16
+            pltpu.make_async_remote_copy(
+                src_ref=es.at[place], dst_ref=es.at[place], send_sem=e_send, recv_sem=e_recv,
+                device_id={'seg': peer // 4, 'col': peer % 4}, device_id_type=MESH).start()
+
+    def cross_event(zb, k, pass_on):
+        ch = chunk(1 - y, zb, k)
+        arrive(ch)
+        if pass_on:
+            onward(zb, ch)
+        send(TWIN, ch)
+
+    def schedule(u):
+        k4 = u % 4
+        v = u + 8
+        along_corner = jnp.where(u < 12, chunk(y, line(u // 4), k4), chunk(1 - y, line(u - 12), LAST))
+        along_middle = jnp.where(u < 8, chunk(y, jnp.where(u < 4, near, far), k4),
+                                 jnp.where(u == 8, chunk(1 - y, near, 2), chunk(1 - y, far, u - 9)))
+        side_corner = chunk(1 - y, jnp.where(u < 13, line(v // 3 - 4), far), jnp.where(u < 13, v % 3, LAST))
+        side_middle = jnp.where(
+            u < 8, chunk(1 - y, jnp.where(u % 2 == 0, near, other), v // 2 - 6),
+            jnp.where(u < 10, chunk(1 - y, other, u - 6), chunk(1 - y, jnp.where(u == 10, near, far), LAST)))
+        side = jnp.where(u < 4, chunk(1 - y, z, u), jnp.where(corner, side_corner, side_middle))
+        return jnp.where(corner, along_corner, along_middle), side
+
+    def cross_opens(u):
+        return (u == 0) | (u == 4) | (corner & ((u == 7) | (u == 10))) | (~corner & ((u == 5) | (u == 9)))
+
+    def evaluate(chunks):
+        pairs(chunks, [ch % PARTS for ch in chunks])
+
+    def from_twin(u):
+        along, side = (ch + plane for ch in schedule(u))
+
+        @pl.when((u == 0) | (u == 4) | (corner & (u == 8)))
+        def _():
+            aq_arrive(block_of(along))
+
+        @pl.when(cross_opens(u))
+        def _():
+            aq_arrive(block_of(jnp.where(~corner & (u == 9), along, side)))
+
+        arrive(along)
+        arrive(side)
+        evaluate([along, side])
 
     def step(u, carry):
-        k4 = u % 4
+        @pl.when(u == 0)
+        def _():
+            evaluate([own + plane + 2, own + plane + 3])
+
+        @pl.when((u > 0) & (corner | (u < 13)))
+        def _():
+            from_twin(u - 1)
+
+        @pl.when(corner & (u == 12))
+        def _():
+            es[place] = e_acc[...]
+
+        along, side = schedule(u)
+
         @pl.when(corner & (u < 12))
         def _():
-            line_event(line(u // 4), k4)
+            line_event(line(u // 4), u % 4)
 
         @pl.when(corner & (u >= 12))
         def _():
-            ch = chunk(1 - y, line(u - 12), LAST)
-            arrive(ch)
-            send(TWIN, ch)
+            cross_event(line(u - 12), LAST, False)
 
         @pl.when(~corner & (u < 4))
         def _():
-            line_event(near, k4)
-            line_event(other, k4)
+            line_event(near, u)
+            line_event(other, u)
 
         @pl.when(~corner & (u >= 4) & (u < 8))
         def _():
-            line_event(far, k4)
+            line_event(far, u - 4)
 
         @pl.when(~corner & (u == 7))
         def _():
@@ -194,75 +292,70 @@
             send_if(z == 1, DOWN, ch)
             send_if(z == 2, UP, ch)
 
-        @pl.when(~corner & (u >= 8) & (u < 11))
-        def _():
-            zb = line(u - 8)
-            ch = chunk(1 - y, zb, LAST)
+        @pl.when(~corner & ((u == 6) | (u == 7)))
+        def _():
+            cross_event(other, u - 4, True)
+
+        @pl.when(~corner & (u == 9))
+        def _():
+            cross_event(near, LAST, True)
+
+        @pl.when(~corner & (u == 11))
+        def _():
+            cross_event(far, 2, False)
+            cross_event(far, LAST, False)
+
+        @pl.when(corner | (u < 11))
+        def _():
+            ch = jnp.where(~corner & (u >= 8), along, side)
             arrive(ch)
-            @pl.when(u < 10)
-            def _():
-                onward(zb, ch)
             send(TWIN, ch)
 
-        side_zb = jnp.where(u < 4, z, jnp.where(u < 13, line((u - 4 + 3 * 4) // 3 - 4), far))
-        side_k = jnp.where(u < 4, u, jnp.where(u < 13, (u - 4 + 3 * 4) % 3, LAST))
-        side = chunk(1 - y, side_zb, side_k)
-
-        @pl.when(corner | (u < 13))
-        def _():
-            arrive(side)
-            send(TWIN, side)
-
-        @pl.when(u == 3)
+        @pl.when((u == 3) | (corner & (u == 2)))
         def _():
             send_if(z < 2, UP, side)
             send_if(z >= 2, DOWN, side)
 
-        @pl.when((u == 0) | (u == 4) | (u == 7) | (u == 10))
-        def _():
-            blk = block_of(side)
+        @pl.when(cross_opens(u))
+        def _():
+            blk = block_of(jnp.where(~corner & (u == 9), along, side))
             aq_arrive(blk)
             aq_send_to(TWIN, blk)
 
-        along = jnp.where(u < 12, chunk(y, line(u // 4), k4), chunk(1 - y, line(u - 12), LAST))
-        pairs_of_step(u, along, side, carry)
-        return along, side
-
-    def from_twin(u, along, side):
-        @pl.when((u == 0) | (u == 4) | (u == 8))
-        def _():
-            aq_arrive(block_of(along))
-
-        @pl.when((u == 0) | (u == 4) | (u == 7) | (u == 10))
-        def _():
-            aq_arrive(block_of(side))
-
-        arrive(along)
-        arrive(side)
-
-    def pairs_of_step(u, along, side, before):
-        along_before, side_before = (ch + plane for ch in before)
-
-        @pl.when(u > 0)
-        def _():
-            from_twin(u - 1, along_before, side_before)
-
-        chunks = [along, side, along_before, side_before]
-        pairs(chunks, [ch % PARTS for ch in chunks])
-
-    along, side = lax.fori_loop(0, 14, step, (own + 2, own + 3))
-    from_twin(13, along + plane, side + plane)
-    pairs([along + plane, side + plane], [along % PARTS, side % PARTS])
-
-    place = seg * 4 + z
-    tile_sum = jnp.sum(row_sum[...].reshape(rows // 8, 8, LANES), axis=0)
-    es[place] = tile_sum
-    def e_copy(peer):
-        return pltpu.make_async_remote_copy(
-            src_ref=es.at[place], dst_ref=es.at[place], send_sem=e_send, recv_sem=e_recv,
-            device_id={'seg': peer // 4, 'col': peer % 4}, device_id_type=MESH)
-    for d in range(1, 16):
-        e_copy((place + d) % 16).start()
+        pl.when(corner & (u == 12))(send_energy)
+
+        @pl.when(corner | (u < 12))
+        def _():
+            evaluate([along, side])
+
+        @pl.when(~corner & ((u == 1) | (u == 3)))
+        def _():
+            pair = [chunk(y, other, u - 1), chunk(y, other, u)]
+
+            @pl.when(u == 1)
+            def _():
+                aq_arrive(block_of(pair[0] + plane))
+
+            for ch in pair:
+                arrive(ch + plane)
+            evaluate(pair + [ch + plane for ch in pair])
+
+        pl.when(~corner & (u == 8))(end_vectors)
+        pl.when(~corner & (u >= 10))(lambda: end_energy(u - 10))
+        return carry
+
+    lax.fori_loop(0, 14, step, 0)
+    pl.when(corner)(lambda: from_twin(13))
+
+    @pl.when(~corner)
+    def _():
+        es[place] = e_acc[...]
+
+    def drain(sem, ref):
+        pltpu.make_async_copy(ref, ref, sem).wait()
+
+    drain(send_sem.at[TWIN], xs.at[pl.ds(0, 8 * PARTS)])
+    pl.when(~corner)(send_energy)
 
     inv_len2 = 1.0 / feat
     for r in range(PARTS):
@@ -270,13 +363,9 @@
         full = jnp.sum(row_sum[span, :], axis=1, keepdims=True)
         out_ref[span, :] = (full * xs[own + r].astype(jnp.float32) - force[span, :]) * inv_len2
 
-    def drain(sem, ref):
-        pltpu.make_async_copy(ref, ref, sem).wait()
-
-    drain(send_sem.at[TWIN], xs.at[pl.ds(0, 8 * PARTS)])
     drain(aq_send.at[TWIN], aq.at[pl.ds(0, 8)])
     drain(aq_send.at[SIDE], aq.at[pl.ds(0, 4)])
-    for zz, counts in enumerate(((0, 5, 14), (14, 10, 13), (10, 14, 13), (5, 0, 14))):
+    for zz, counts in enumerate(((0, 6, 14), (14, 11, 11), (11, 14, 11), (6, 0, 14))):
         @pl.when(z == zz)
         def _():
             for way, count in zip((DOWN, UP, SIDE), counts):
@@ -288,7 +377,7 @@
                 drain(aq_send.at[UP], aq.at[pl.ds(0, zz + 1)])
     drain(e_recv, es.at[pl.ds(0, 15)])
     drain(e_send, es.at[pl.ds(0, 15)])
-    e_ref[0] = 0.5 * jnp.sum(es[...])
+    e_ref[0] = jnp.sum(es[...])
 
 
 def solution(mesh):
@@ -308,12 +397,13 @@
             out_specs=(pl.BlockSpec(memory_space=vmem), pl.BlockSpec(memory_space=pltpu.SMEM)),
             scratch_shapes=[
                 vmem((16 * PARTS, part, feat), bf16), vmem((16, 2 * groups, LANES), f32), vmem((16, 8, LANES), f32),
-                vmem((groups, LANES), f32),
-                vmem((rows, LANES), f32), vmem((rows, LANES), f32), vmem((rows, feat), f32), vmem((rows, LANES), f32),
+                vmem((8, LANES), f32), vmem((groups, LANES), f32),
+                vmem((rows, LANES), f32), vmem((rows, LANES), f32), vmem((rows, LANES), f32), vmem((rows, LANES), f32),
+                vmem((rows, feat), f32), vmem((rows, LANES), f32),
                 dma((PARTS + 1,)), dma((16 * PARTS,)), dma((16,)), dma, dma((4,)), dma((4,)), dma],
             compiler_params=pltpu.CompilerParams(
                 collective_id=0, has_side_effects=True, vmem_limit_bytes=40 * 2 ** 20),
-        )(x_own, q_own.reshape(groups, LANES))
+        )(*(pltpu.with_memory_space_constraint(v, pltpu.HBM) for v in (x_own, q_own.reshape(groups, LANES))))
 
     row_spec = P(ROW_AXES, None)
     return jax.shard_map(per_device, mesh=mesh, in_specs=(row_spec, P(ROW_AXES)),

time: 61.5 us -> 57.1 us (0.928)
  Pallas kernels: 56.2 us -> 53.6 us
  local copies, waits for them, and re-layouts: 2.69 us -> 0.97 us
    pallas_call x1, Pallas kernels: 56.2 us -> 53.6 us  [per_device(): pl.pallas_call(pair_kernel, out_shape=(jax.ShapeDtypeStruct((rows, feat),...]
    unnamed x5 -> x1, local copies, waits for them, and re-layouts: 2.69 us -> 0.97 us
where the time goes in v3:
time: 57.1 us; the launch traced here: 56.9 us
  Pallas kernels  53.6 us (94%)
  between operations  2.33 us (4%)
  local copies, waits for them, and re-layouts  0.97 us (2%)
    pallas_call x1, Pallas kernels, per_device(): pl.pallas_call(pair_kernel, out_shape=(jax.ShapeDtypeStruct((rows, feat),...  53.6 us

profile of v3, /device:TPU:0, one launch (start us, length us, event | category | flops | bytes accessed | tf_op | source)
XLA Modules:
  0.0 56.9 jit_solution(8148821542667955781)
XLA Ops:
  0.6 53.6 %shard_map.41 = (f32[1024,256]{1,0:T(8,128)S(1)}, f32[1]{0:T(128)}) custom-call(bf16[1024,256]{1,0:T(8,128)(2,1)} %x_hbm.1, f32[8,128]{1,0:T(8,128)} %bitcast.1), custom_call_target="tpu_custom_call" | custom-call | tf_op jit(solution)/shard_map/pallas_call | solution.py:393
  54.3 1.0 %copy.6 = f32[1024,256]{1,0:T(8,128)} copy(f32[1024,256]{1,0:T(8,128)S(1)} %get-tuple-element.4) | data formatting | bytes 2097152

commit v4 on v3

--- a/solution.py
+++ b/solution.py
@@ -180,8 +180,8 @@
         for r in range(PARTS):
             tile(r, chunks, parts_of, masked)
 
-    end_rows = chunk(y, 0, 0)
-    end_cols = ((2 * (1 - y) + z - 1) * 4 + 3) * PARTS
+    end_rows = chunk(y, far, 0)
+    end_cols = chunk(1 - y, other, 0) + jnp.where(z == 1, 0, plane)
 
     def end_vectors():
         blk = block_of(end_rows)
@@ -263,7 +263,7 @@
         def _():
             from_twin(u - 1)
 
-        @pl.when(corner & (u == 12))
+        @pl.when(u == 12)
         def _():
             es[place] = e_acc[...]
 
@@ -322,7 +322,7 @@
             aq_arrive(blk)
             aq_send_to(TWIN, blk)
 
-        pl.when(corner & (u == 12))(send_energy)
+        pl.when(u == jnp.where(corner, 12, 13))(send_energy)
 
         @pl.when(corner | (u < 12))
         def _():
@@ -340,22 +340,17 @@
                 arrive(ch + plane)
             evaluate(pair + [ch + plane for ch in pair])
 
-        pl.when(~corner & (u == 8))(end_vectors)
-        pl.when(~corner & (u >= 10))(lambda: end_energy(u - 10))
+        pl.when(~corner & (u == 6))(end_vectors)
+        pl.when(~corner & (u >= 7) & (u < 11))(lambda: end_energy(u - 7))
         return carry
 
     lax.fori_loop(0, 14, step, 0)
     pl.when(corner)(lambda: from_twin(13))
 
-    @pl.when(~corner)
-    def _():
-        es[place] = e_acc[...]
-
     def drain(sem, ref):
         pltpu.make_async_copy(ref, ref, sem).wait()
 
     drain(send_sem.at[TWIN], xs.at[pl.ds(0, 8 * PARTS)])
-    pl.when(~corner)(send_energy)
 
     inv_len2 = 1.0 / feat
     for r in range(PARTS):

time: 57.1 us -> 56.9 us (level)
  no operation moved by 1% of the time
where the time goes in v4:
time: 56.9 us; the launch traced here: 56.7 us
  Pallas kernels  53.4 us (94%)
  between operations  2.33 us (4%)
  local copies, waits for them, and re-layouts  0.97 us (2%)
    pallas_call x1, Pallas kernels, per_device(): pl.pallas_call(pair_kernel, out_shape=(jax.ShapeDtypeStruct((rows, feat),...  53.4 us

profile of v4, /device:TPU:0, one launch (start us, length us, event | category | flops | bytes accessed | tf_op | source)
XLA Modules:
  0.0 56.7 jit_solution(16504736179486133231)
XLA Ops:
  0.6 53.4 %shard_map.41 = (f32[1024,256]{1,0:T(8,128)S(1)}, f32[1]{0:T(128)}) custom-call(bf16[1024,256]{1,0:T(8,128)(2,1)} %x_hbm.1, f32[8,128]{1,0:T(8,128)} %bitcast.1), custom_call_target="tpu_custom_call" | custom-call | tf_op jit(solution)/shard_map/pallas_call | solution.py:388
  54.0 1.0 %copy.6 = f32[1024,256]{1,0:T(8,128)} copy(f32[1024,256]{1,0:T(8,128)S(1)} %get-tuple-element.4) | data formatting | bytes 2097152

commit v5 on v4

--- a/solution.py
+++ b/solution.py
@@ -252,30 +252,13 @@
 
         arrive(along)
         arrive(side)
-        evaluate([along, side])
 
     def step(u, carry):
-        @pl.when(u == 0)
-        def _():
-            evaluate([own + plane + 2, own + plane + 3])
-
-        @pl.when((u > 0) & (corner | (u < 13)))
-        def _():
-            from_twin(u - 1)
-
-        @pl.when(u == 12)
-        def _():
-            es[place] = e_acc[...]
-
         along, side = schedule(u)
 
-        @pl.when(corner & (u < 12))
+        @pl.when(corner)
         def _():
             line_event(line(u // 4), u % 4)
-
-        @pl.when(corner & (u >= 12))
-        def _():
-            cross_event(line(u - 12), LAST, False)
 
         @pl.when(~corner & (u < 4))
         def _():
@@ -322,11 +305,12 @@
             aq_arrive(blk)
             aq_send_to(TWIN, blk)
 
-        pl.when(u == jnp.where(corner, 12, 13))(send_energy)
-
-        @pl.when(corner | (u < 12))
-        def _():
-            evaluate([along, side])
+        @pl.when(u > 0)
+        def _():
+            from_twin(u - 1)
+
+        before = schedule(jnp.maximum(u - 1, 0))
+        evaluate([along, side] + [jnp.where(u > 0, ch, own + 2 + n) + plane for n, ch in enumerate(before)])
 
         @pl.when(~corner & ((u == 1) | (u == 3)))
         def _():
@@ -344,8 +328,36 @@
         pl.when(~corner & (u >= 7) & (u < 11))(lambda: end_energy(u - 7))
         return carry
 
-    lax.fori_loop(0, 14, step, 0)
-    pl.when(corner)(lambda: from_twin(13))
+    lax.fori_loop(0, 12, step, 0)
+
+    def last_steps(i, carry):
+        u = 11 + (i + 1) // 2
+        along, side = schedule(u)
+        twin = i % 2 == 0
+
+        @pl.when(i == 1)
+        def _():
+            es[place] = e_acc[...]
+
+        @pl.when(corner & ~twin)
+        def _():
+            cross_event(line(u - 12), LAST, False)
+            arrive(side)
+            send(TWIN, side)
+
+        pl.when(i == 1)(send_energy)
+
+        @pl.when((corner | (i == 0)) & twin)
+        def _():
+            from_twin(u)
+
+        @pl.when(corner | (i == 0))
+        def _():
+            evaluate([ch + jnp.where(twin, plane, 0) for ch in (along, side)])
+
+        return carry
+
+    lax.fori_loop(0, 5, last_steps, 0)
 
     def drain(sem, ref):
         pltpu.make_async_copy(ref, ref, sem).wait()

time: 56.9 us -> 54.3 us (0.954)
  Pallas kernels: 53.4 us -> 50.9 us
    pallas_call x1, Pallas kernels: 53.4 us -> 50.9 us  [per_device(): pl.pallas_call(pair_kernel, out_shape=(jax.ShapeDtypeStruct((rows, feat),...]
where the time goes in v5:
time: 54.3 us; the launch traced here: 54.2 us
  Pallas kernels  50.9 us (94%)
  between operations  2.33 us (4%)
  local copies, waits for them, and re-layouts  0.97 us (2%)
    pallas_call x1, Pallas kernels, per_device(): pl.pallas_call(pair_kernel, out_shape=(jax.ShapeDtypeStruct((rows, feat),...  50.9 us

profile of v5, /device:TPU:0, one launch (start us, length us, event | category | flops | bytes accessed | tf_op | source)
XLA Modules:
  0.0 54.2 jit_solution(11521941557859725390)
XLA Ops:
  0.6 50.9 %shard_map.41 = (f32[1024,256]{1,0:T(8,128)S(1)}, f32[1]{0:T(128)}) custom-call(bf16[1024,256]{1,0:T(8,128)(2,1)} %x_hbm.1, f32[8,128]{1,0:T(8,128)} %bitcast.1), custom_call_target="tpu_custom_call" | custom-call | tf_op jit(solution)/shard_map/pallas_call | solution.py:400
  51.5 1.0 %copy.6 = f32[1024,256]{1,0:T(8,128)} copy(f32[1024,256]{1,0:T(8,128)S(1)} %get-tuple-element.4) | data formatting | bytes 2097152

commit v6 on v5

--- a/solution.py
+++ b/solution.py
@@ -16,7 +16,7 @@
 
 
 def pair_kernel(x_hbm, q_hbm, out_ref, e_ref, xs, aq, es, e_acc, q_ref, a_col, q_col,
-                a_end, q_end, force, row_sum,
+                a_end, q_end, force, row_sum, low,
                 load_sem, recv_sem, aq_recv, e_recv, send_sem, aq_send, e_send):
     rows, feat = x_hbm.shape
     part = rows // PARTS
@@ -107,38 +107,41 @@
     greet(SIDE)
     greet(TWIN)
 
+    def send_own(k):
+        send_if(z > 0, DOWN, own + k)
+        send_if(z < 3, UP, own + k)
+        send(SIDE, own + k)
+        send(TWIN, own + k)
+
+    loads[0].wait()
+    pl.semaphore_wait(barrier, jnp.where(corner, 3, 4))
+    send_own(0)
+
     own_blk = block_of(own)
-    loads[PARTS].wait()
-    for k in range(PARTS):
-        loads[k].wait()
-        wide = xs[own + k].astype(jnp.float32)
-        a_col[pl.ds(k * part, part), :] = jnp.broadcast_to(
-            scale * jnp.sum(wide * wide, axis=1, keepdims=True), (part, LANES))
+    for load in loads[1:]:
+        load.wait()
+    wide = xs[pl.ds(own, PARTS)].reshape(rows, feat).astype(jnp.float32)
+    a_col[...] = jnp.broadcast_to(scale * jnp.sum(wide * wide, axis=1, keepdims=True), (rows, LANES))
     for g in range(groups):
         span = pl.ds(g * LANES, LANES)
         aq[own_blk, g:g + 1, :] = jnp.transpose(a_col[span, :])[0:1, :]
         aq[own_blk, groups + g:groups + g + 1, :] = q_ref[g:g + 1, :]
-        q_col[span, :] = jnp.transpose(jnp.broadcast_to(q_ref[g:g + 1, :], (LANES, LANES)))
-
-    pl.semaphore_wait(barrier, jnp.where(corner, 3, 4))
-    for k in range(PARTS):
-        send_if(z > 0, DOWN, own + k)
-        send_if(z < 3, UP, own + k)
-        send(SIDE, own + k)
-        send(TWIN, own + k)
-        if k == 0:
-            aq_send_if(z > 0, DOWN, own_blk)
-            aq_send_if(z < 3, UP, own_blk)
-            aq_send_to(SIDE, own_blk)
-            aq_send_to(TWIN, own_blk)
+
+    aq_send_if(z > 0, DOWN, own_blk)
+    aq_send_if(z < 3, UP, own_blk)
+    aq_send_to(SIDE, own_blk)
+    aq_send_to(TWIN, own_blk)
+    for k in range(1, PARTS):
+        send_own(k)
+    for g in range(groups):
+        q_col[pl.ds(g * LANES, LANES), :] = jnp.transpose(jnp.broadcast_to(q_ref[g:g + 1, :], (LANES, LANES)))
     force[...] = jnp.zeros_like(force)
     row_sum[...] = jnp.zeros_like(row_sum)
     e_acc[...] = jnp.zeros_like(e_acc)
 
     def share(ch):
-        same_line = (block_of(ch) // 8) == y
         z_j = block_of(ch) % 4
-        at_corner = jnp.where((z_j == z) | ((z_j == far) & same_line), 0.5, 0.0)
+        at_corner = jnp.where(z_j == z, 0.5, 0.0)
         at_middle = jnp.where((z_j == 1) | (z_j == 2), 0.5, 1.0)
         return jnp.where(corner, at_corner, at_middle)
 
@@ -155,33 +158,31 @@
         return weights[:, :LANES] + weights[:, LANES:]
 
     def stack(halves):
-        return jnp.sum(halves.reshape(part // 8, 8, LANES), axis=0)
-
-    def tile(r, chunks, parts_of, masked):
-        span = pl.ds(r * part, part)
-        acc = force[span, :]
-        total = row_sum[span, :]
+        return jnp.sum(halves.reshape(halves.shape[0] // 8, 8, LANES), axis=0)
+
+    def pairs(chunks, parts_of, masked=False):
+        x_own = xs[pl.ds(own, PARTS)].reshape(rows, feat)
+        total = row_sum[...]
         e_part = jnp.zeros((8, LANES), jnp.float32)
         for n, (ch, k) in enumerate(zip(chunks, parts_of)):
-            weights = weights_of(xs[own + r], a_col[span, :], q_col[span, :], ch, k)
-            if masked and n == r:
+            weights = weights_of(x_own, a_col[...], q_col[...], ch, k)
+            if masked:
                 rid = lax.broadcasted_iota(jnp.int32, weights.shape, 0)
                 cid = lax.broadcasted_iota(jnp.int32, weights.shape, 1)
-                weights = jnp.where(rid == cid, 0.0, weights)
+                weights = jnp.where(rid == cid + n * part, 0.0, weights)
             halves = fold(weights)
             total = total + halves
             e_part = e_part + share(ch) * stack(halves)
-            acc = acc + jnp.dot(weights.astype(jnp.bfloat16), xs[ch], preferred_element_type=jnp.float32)
-        force[span, :] = acc
-        row_sum[span, :] = total
+            low[:, pl.ds(n * part, part)] = weights.astype(jnp.bfloat16)
+        row_sum[...] = total
         e_acc[...] += e_part
-
-    def pairs(chunks, parts_of, masked=False):
-        for r in range(PARTS):
-            tile(r, chunks, parts_of, masked)
+        acc = force[...]
+        for n, ch in enumerate(chunks):
+            acc = acc + jnp.dot(low[:, pl.ds(n * part, part)], xs[ch], preferred_element_type=jnp.float32)
+        force[...] = acc
 
     end_rows = chunk(y, far, 0)
-    end_cols = chunk(1 - y, other, 0) + jnp.where(z == 1, 0, plane)
+    end_cols = [chunk(yy, other, 0) + jnp.where(z == 1, 0, plane) for yy in (y, 1 - y)]
 
     def end_vectors():
         blk = block_of(end_rows)
@@ -192,10 +193,9 @@
 
     def end_energy(k):
         e_part = jnp.zeros((8, LANES), jnp.float32)
-        for r in range(PARTS):
-            span = pl.ds(r * part, part)
-            e_part = e_part + stack(fold(weights_of(
-                xs[end_rows + r], a_end[span, :], q_end[span, :], end_cols + k, k)))
+        x_end = xs[pl.ds(end_rows, PARTS)].reshape(rows, feat)
+        for cols in end_cols:
+            e_part = e_part + stack(fold(weights_of(x_end, a_end[...], q_end[...], cols + k, k)))
         e_acc[...] += e_part
 
     pairs([own + k for k in range(PARTS)], range(PARTS), masked=True)
@@ -324,6 +324,11 @@
                 arrive(ch + plane)
             evaluate(pair + [ch + plane for ch in pair])
 
+        @pl.when(corner & (u == 6))
+        def _():
+            es[place] = e_acc[...]
+
+        pl.when(corner & (u == 8))(send_energy)
         pl.when(~corner & (u == 6))(end_vectors)
         pl.when(~corner & (u >= 7) & (u < 11))(lambda: end_energy(u - 7))
         return carry
@@ -335,7 +340,7 @@
         along, side = schedule(u)
         twin = i % 2 == 0
 
-        @pl.when(i == 1)
+        @pl.when(~corner & (i == 1))
         def _():
             es[place] = e_acc[...]
 
@@ -345,7 +350,7 @@
             arrive(side)
             send(TWIN, side)
 
-        pl.when(i == 1)(send_energy)
+        pl.when(~corner & (i == 1))(send_energy)
 
         @pl.when((corner | (i == 0)) & twin)
         def _():
@@ -406,7 +411,7 @@
                 vmem((16 * PARTS, part, feat), bf16), vmem((16, 2 * groups, LANES), f32), vmem((16, 8, LANES), f32),
                 vmem((8, LANES), f32), vmem((groups, LANES), f32),
                 vmem((rows, LANES), f32), vmem((rows, LANES), f32), vmem((rows, LANES), f32), vmem((rows, LANES), f32),
-                vmem((rows, feat), f32), vmem((rows, LANES), f32),
+                vmem((rows, feat), f32), vmem((rows, LANES), f32), vmem((rows, rows), bf16),
                 dma((PARTS + 1,)), dma((16 * PARTS,)), dma((16,)), dma, dma((4,)), dma((4,)), dma],
             compiler_params=pltpu.CompilerParams(
                 collective_id=0, has_side_effects=True, vmem_limit_bytes=40 * 2 ** 20),

time: 54.3 us -> 53.7 us (0.989)
  Pallas kernels: 50.9 us -> 50.2 us
    pallas_call x1, Pallas kernels: 50.9 us -> 50.2 us  [per_device(): pl.pallas_call(pair_kernel, out_shape=(jax.ShapeDtypeStruct((rows, feat),...]
where the time goes in v6:
time: 53.7 us; the launch traced here: 53.5 us
  Pallas kernels  50.2 us (93%)
  between operations  2.33 us (4%)
  local copies, waits for them, and re-layouts  0.97 us (2%)
    pallas_call x1, Pallas kernels, per_device(): pl.pallas_call(pair_kernel, out_shape=(jax.ShapeDtypeStruct((rows, feat),...  50.2 us

profile of v6, /device:TPU:0, one launch (start us, length us, event | category | flops | bytes accessed | tf_op | source)
XLA Modules:
  0.0 53.5 jit_solution(11894493827944600732)
XLA Ops:
  0.6 50.2 %shard_map.41 = (f32[1024,256]{1,0:T(8,128)S(1)}, f32[1]{0:T(128)}) custom-call(bf16[1024,256]{1,0:T(8,128)(2,1)} %x_hbm.1, f32[8,128]{1,0:T(8,128)} %bitcast.1), custom_call_target="tpu_custom_call" | custom-call | tf_op jit(solution)/shard_map/pallas_call | solution.py:405
  50.8 1.0 %copy.6 = f32[1024,256]{1,0:T(8,128)} copy(f32[1024,256]{1,0:T(8,128)S(1)} %get-tuple-element.4) | data formatting | bytes 2097152

commit v7 on v6

--- a/solution.py
+++ b/solution.py
@@ -79,8 +79,8 @@
         ch = chunk(y, zb, k)
         arrive(ch)
         onward(zb, ch)
-        near_side = jnp.where((zb == near) | (corner & (zb == other)), 3, 2)
-        send_if(k < jnp.where(corner & (zb == far), PARTS, near_side), SIDE, ch)
+        limit = jnp.where(corner, jnp.where(zb == other, PARTS, 3), jnp.where(zb == near, 3, 2))
+        send_if(k < limit, SIDE, ch)
         send(TWIN, ch)
 
         @pl.when(k == 0)
@@ -222,19 +222,19 @@
 
     def schedule(u):
         k4 = u % 4
-        v = u + 8
-        along_corner = jnp.where(u < 12, chunk(y, line(u // 4), k4), chunk(1 - y, line(u - 12), LAST))
+        along_corner = jnp.where(u < 12, chunk(y, line(u // 4), k4), chunk(1 - y, jnp.where(u == 12, near, far), LAST))
         along_middle = jnp.where(u < 8, chunk(y, jnp.where(u < 4, near, far), k4),
                                  jnp.where(u == 8, chunk(1 - y, near, 2), chunk(1 - y, far, u - 9)))
-        side_corner = chunk(1 - y, jnp.where(u < 13, line(v // 3 - 4), far), jnp.where(u < 13, v % 3, LAST))
+        side_corner = jnp.where(u < 7, chunk(1 - y, near, u - 4),
+                                jnp.where(u < 11, chunk(1 - y, other, u - 7), chunk(1 - y, far, u - 11)))
         side_middle = jnp.where(
-            u < 8, chunk(1 - y, jnp.where(u % 2 == 0, near, other), v // 2 - 6),
+            u < 8, chunk(1 - y, jnp.where(u % 2 == 0, near, other), u // 2 - 2),
             jnp.where(u < 10, chunk(1 - y, other, u - 6), chunk(1 - y, jnp.where(u == 10, near, far), LAST)))
         side = jnp.where(u < 4, chunk(1 - y, z, u), jnp.where(corner, side_corner, side_middle))
         return jnp.where(corner, along_corner, along_middle), side
 
     def cross_opens(u):
-        return (u == 0) | (u == 4) | (corner & ((u == 7) | (u == 10))) | (~corner & ((u == 5) | (u == 9)))
+        return (u == 0) | (u == 4) | (corner & ((u == 7) | (u == 11))) | (~corner & ((u == 5) | (u == 9)))
 
     def evaluate(chunks):
         pairs(chunks, [ch % PARTS for ch in chunks])
@@ -281,18 +281,21 @@
 
         @pl.when(~corner & (u == 9))
         def _():
-            cross_event(near, LAST, True)
+            cross_event(near, LAST, False)
 
         @pl.when(~corner & (u == 11))
         def _():
             cross_event(far, 2, False)
-            cross_event(far, LAST, False)
 
         @pl.when(corner | (u < 11))
         def _():
             ch = jnp.where(~corner & (u >= 8), along, side)
             arrive(ch)
             send(TWIN, ch)
+
+        @pl.when(~corner & (u == 10))
+        def _():
+            cross_event(far, LAST, True)
 
         @pl.when((u == 3) | (corner & (u == 2)))
         def _():
@@ -336,33 +339,37 @@
     lax.fori_loop(0, 12, step, 0)
 
     def last_steps(i, carry):
-        u = 11 + (i + 1) // 2
-        along, side = schedule(u)
-        twin = i % 2 == 0
-
         @pl.when(~corner & (i == 1))
         def _():
             es[place] = e_acc[...]
 
-        @pl.when(corner & ~twin)
-        def _():
-            cross_event(line(u - 12), LAST, False)
+        @pl.when(corner & (i > 0))
+        def _():
+            cross_event(jnp.where(i == 1, near, far), LAST, False)
+            side = schedule(11 + i)[1]
             arrive(side)
             send(TWIN, side)
 
         pl.when(~corner & (i == 1))(send_energy)
 
-        @pl.when((corner | (i == 0)) & twin)
-        def _():
-            from_twin(u)
-
         @pl.when(corner | (i == 0))
         def _():
-            evaluate([ch + jnp.where(twin, plane, 0) for ch in (along, side)])
+            @pl.when(i == 0)
+            def _():
+                from_twin(11)
+
+            @pl.when(i == 2)
+            def _():
+                from_twin(12)
+                evaluate(list(schedule(13)) + [ch + plane for ch in schedule(12)])
+                from_twin(13)
+
+            u = jnp.where(i == 0, 11, 11 + i)
+            evaluate([ch + jnp.where(i == 1, 0, plane) for ch in schedule(u)])
 
         return carry
 
-    lax.fori_loop(0, 5, last_steps, 0)
+    lax.fori_loop(0, 3, last_steps, 0)
 
     def drain(sem, ref):
         pltpu.make_async_copy(ref, ref, sem).wait()

time: 53.7 us -> 53.4 us (level)
  no operation moved by 1% of the time
where the time goes in v7:
time: 53.4 us; the launch traced here: 53.2 us
  Pallas kernels  49.9 us (93%)
  between operations  2.33 us (4%)
  local copies, waits for them, and re-layouts  0.97 us (2%)
    pallas_call x1, Pallas kernels, per_device(): pl.pallas_call(pair_kernel, out_shape=(jax.ShapeDtypeStruct((rows, feat),...  49.9 us

profile of v7, /device:TPU:0, one launch (start us, length us, event | category | flops | bytes accessed | tf_op | source)
XLA Modules:
  0.0 53.2 jit_solution(16680997272820956072)
XLA Ops:
  0.6 49.9 %shard_map.41 = (f32[1024,256]{1,0:T(8,128)S(1)}, f32[1]{0:T(128)}) custom-call(bf16[1024,256]{1,0:T(8,128)(2,1)} %x_hbm.1, f32[8,128]{1,0:T(8,128)} %bitcast.1), custom_call_target="tpu_custom_call" | custom-call | tf_op jit(solution)/shard_map/pallas_call | solution.py:412
  50.5 1.0 %copy.6 = f32[1024,256]{1,0:T(8,128)} copy(f32[1024,256]{1,0:T(8,128)S(1)} %get-tuple-element.4) | data formatting | bytes 2097152
